TPU v7x, 32 devices: a whole 2x2x4 slice. The times are simulated.
32 devices in a mesh: job: 4 (over y, x), zero: 2 (over core), cols: 4 (over z).
Axes of the slice: x: 2, y: 2, z: 4, core: 2. Of those that a mesh axis runs over, the one named last changes fastest.
Arguments:
- weight_gate: bfloat16 [8192, 8192], P(('job', 'zero'), 'cols'), parts along dimension 0, may hold values from -0.1875 to 0.1875
- low_gate: bfloat16 [8192, 32], P(('job', 'zero')), parts along dimension 0, may hold values from -0.125 to 0.125
- high_gate: bfloat16 [128, 8192], P('job', 'cols'), parts along dimension 0, may hold values from -1 to 1
- weight_up: bfloat16 [8192, 8192], P(('job', 'zero'), 'cols'), parts along dimension 0, may hold values from -0.1875 to 0.1875
- low_up: bfloat16 [8192, 32], P(('job', 'zero')), parts along dimension 0, may hold values from -0.125 to 0.125
- high_up: bfloat16 [128, 8192], P('job', 'cols'), parts along dimension 0, may hold values from -1 to 1
- norm_train: float32 [8192], P(('job', 'zero', 'cols')), parts along dimension 0, may hold values from 0.25 to 1.75
- norm_step: float32 [8192], P(('job', 'zero', 'cols')), parts along dimension 0, may hold values from -0.3 to 0.3
Outputs:
- serving_gate: bfloat16 [8192, 8192], P('job', 'cols'), parts along dimension 0
- serving_up: bfloat16 [8192, 8192], P('job', 'cols'), parts along dimension 0
- column_gate: float32 [32768], P(('job', 'cols')), parts along dimension 0
- column_up: float32 [32768], P(('job', 'cols')), parts along dimension 0
- serve_norm: bfloat16 [8192], P('job'), parts along dimension 0
There are 4 independent parts, one for each index of `job`. A program takes and returns all parts, laid end to end along the dimension named above; each array names one. Nothing has to cross between parts.
All inputs are finite; a program needn't handle non-finite values. Where the computation divides by a largest or mean magnitude, that divisor is 1e-20 or more.
Results may differ from a plain program's by a relative error of at most 0.001.
Values may be sent and summed in bfloat16 or wider, within the bound.
A program may use at most 128 MiB of HBM per device.

v0:
```python
import functools

import jax
import jax.numpy as jnp
from jax import lax
from jax.experimental import pallas as pl
from jax.experimental.pallas import tpu as pltpu
from jax.sharding import PartitionSpec as P

mix_rate = 2.0
MESH = pl.DeviceIdType.MESH


def first_kernel(zeros, cols, lows, weight_ref, *refs):
    train_ref, step_ref = refs[:2]
    low_refs = refs[2:2 + lows]
    norm_ref = refs[2 + lows]
    got_refs = refs[3 + lows:3 + 2 * lows]
    moved_refs = refs[3 + 2 * lows:2 + 2 * lows + zeros]
    refs = refs[2 + 2 * lows + zeros:]
    landed = refs[:lows]
    mine, slots, norm_send, norm_recv, low_send, low_recv, weight_send, weight_recv = refs[lows:]
    group = zeros * cols
    zero, col = lax.axis_index("zero"), lax.axis_index("cols")
    me = zero * cols + col

    def device(rank):
        return {"zero": rank // cols, "cols": lax.rem(rank, cols)}

    barrier = pltpu.get_barrier_semaphore()
    for s in range(1, group):
        pl.semaphore_signal(barrier, inc=1, device_id=device(lax.rem(me + s, group)), device_id_type=MESH)
    mine[...] = train_ref[...] + step_ref[...]
    pl.semaphore_wait(barrier, group - 1)

    copies = []
    for s in range(1, zeros):
        for k in range(lows):
            copies.append(pltpu.make_async_remote_copy(
                src_ref=low_refs[k], dst_ref=landed[k].at[s - 1],
                send_sem=low_send.at[k, s - 1], recv_sem=low_recv.at[k, s - 1],
                device_id={"zero": lax.rem(zero + s, zeros), "cols": col}, device_id_type=MESH))
            copies[-1].start()
    for s in range(1, zeros):
        copies.append(pltpu.make_async_remote_copy(
            src_ref=weight_ref, dst_ref=moved_refs[s - 1],
            send_sem=weight_send.at[s - 1], recv_sem=weight_recv.at[s - 1],
            device_id={"zero": lax.rem(zero + s, zeros), "cols": col}, device_id_type=MESH))
    for s in range(1, group):
        copy = pltpu.make_async_remote_copy(
            src_ref=mine, dst_ref=slots.at[me],
            send_sem=norm_send.at[s - 1], recv_sem=norm_recv.at[s - 1],
            device_id=device(lax.rem(me + s, group)), device_id_type=MESH)
        copy.start()
        copies.append(copy)
    for copy in copies[lows * (zeros - 1):(1 + lows) * (zeros - 1)]:
        copy.start()
    for k in range(lows):
        got_refs[k][0] = low_refs[k][...].T
    for copy in copies:
        copy.wait()
    for k in range(lows):
        for s in range(1, zeros):
            got_refs[k][s] = landed[k][s - 1].T
    slots[me] = mine[...]
    norm_ref[...] = jnp.concatenate([slots[g] for g in range(group)], axis=0).astype(norm_ref.dtype)


def exchange_first(zeros, cols, weight, train, step, lows):
    group = zeros * cols
    lanes = 128 if train.shape[0] % 128 == 0 else train.shape[0]
    tall = train.shape[0] // lanes
    outs = pl.pallas_call(
        functools.partial(first_kernel, zeros, cols, len(lows)),
        out_shape=[jax.ShapeDtypeStruct((group * tall, lanes), jnp.bfloat16)]
        + [jax.ShapeDtypeStruct((zeros,) + low.shape, low.dtype) for low in lows]
        + [jax.ShapeDtypeStruct(weight.shape, weight.dtype)] * (zeros - 1),
        in_specs=[pl.BlockSpec(memory_space=pl.ANY)] + [pl.BlockSpec(memory_space=pltpu.VMEM)] * (2 + len(lows)),
        out_specs=[pl.BlockSpec(memory_space=pltpu.VMEM)] * (1 + len(lows))
        + [pl.BlockSpec(memory_space=pl.ANY)] * (zeros - 1),
        scratch_shapes=[
            pltpu.VMEM((zeros - 1,) + low.shape[::-1], low.dtype) for low in lows
        ] + [
            pltpu.VMEM((tall, lanes), jnp.float32),
            pltpu.VMEM((group, tall, lanes), jnp.float32),
            pltpu.SemaphoreType.DMA((group - 1,)),
            pltpu.SemaphoreType.DMA((group - 1,)),
            pltpu.SemaphoreType.DMA((len(lows), zeros - 1)),
            pltpu.SemaphoreType.DMA((len(lows), zeros - 1)),
            pltpu.SemaphoreType.DMA((zeros - 1,)),
            pltpu.SemaphoreType.DMA((zeros - 1,)),
        ],
        cost_estimate=pl.CostEstimate(flops=0, bytes_accessed=2 ** 22, transcendentals=0),
        compiler_params=pltpu.CompilerParams(collective_id=0, has_side_effects=True),
    )(weight, train.reshape(tall, lanes), step.reshape(tall, lanes), *[low.T for low in lows])
    return outs[0].reshape(group * tall * lanes), outs[1:1 + len(lows)], outs[1 + len(lows):]


def merge_kernel(zeros, chunk, *refs):
    weight_refs = refs[:zeros]
    low_ref, high_ref, out_ref, column_ref, whole = refs[zeros:]
    zero = lax.axis_index("zero")
    rows, width = weight_refs[0].shape
    high = high_ref[...] * jnp.bfloat16(mix_rate)
    most = jnp.zeros((8, width), jnp.float32)
    for s in range(zeros):
        def step(i, most, s=s):
            at = pl.ds(pl.multiple_of(i * chunk, chunk), chunk)
            low = low_ref[s, at, :]
            value = weight_refs[s][at, :].astype(jnp.float32) + jnp.dot(
                low, high, preferred_element_type=jnp.float32)
            whole[s, at, :] = value
            return jnp.maximum(most, jnp.max(jnp.abs(value).reshape(chunk // 8, 8, width), axis=0))
        most = lax.fori_loop(0, rows // chunk, step, most, unroll=True)
    column = jnp.max(most, axis=0, keepdims=True)
    column_ref[...] = column
    scale = 1.0 / column
    for s in range(zeros):
        base = lax.rem(zero - s + zeros, zeros) * rows

        def put(i, carry, s=s, base=base):
            start = pl.multiple_of(i * chunk, chunk)
            out_ref[pl.ds(pl.multiple_of(base + start, chunk), chunk), :] = (
                whole[s, pl.ds(start, chunk), :] * scale).astype(out_ref.dtype)
            return carry
        lax.fori_loop(0, rows // chunk, put, 0, unroll=True)


def merge(zeros, weights, low, high):
    rows, columns = weights[0].shape
    rank = low.shape[2]
    width = min(512, columns)
    chunk = min(128, rows)
    serving, column = pl.pallas_call(
        functools.partial(merge_kernel, zeros, chunk),
        grid=(columns // width,),
        out_shape=[
            jax.ShapeDtypeStruct((rows * zeros, columns), jnp.bfloat16),
            jax.ShapeDtypeStruct((1, columns), jnp.float32),
        ],
        in_specs=[pl.BlockSpec((rows, width), lambda j: (0, j))] * zeros + [
            pl.BlockSpec((zeros, rows, rank), lambda j: (0, 0, 0)),
            pl.BlockSpec((rank, width), lambda j: (0, j)),
        ],
        out_specs=[
            pl.BlockSpec((rows * zeros, width), lambda j: (0, j)),
            pl.BlockSpec((1, width), lambda j: (0, j)),
        ],
        scratch_shapes=[pltpu.VMEM((zeros, rows, width), jnp.float32)],
        cost_estimate=pl.CostEstimate(
            flops=2 * rows * zeros * columns * rank,
            bytes_accessed=4 * rows * zeros * columns, transcendentals=0),
        compiler_params=pltpu.CompilerParams(dimension_semantics=("arbitrary",), vmem_limit_bytes=60 * 2 ** 20),
    )(*weights, low, high)
    return serving, column.reshape(columns)


def per_device(zeros, cols, weight_gate, low_gate, high_gate, weight_up, low_up, high_up, norm_train, norm_step):
    def moved(array):
        return [array] + [
            lax.ppermute(array, "zero", [(i, (i + s) % zeros) for i in range(zeros)])
            for s in range(1, zeros)
        ]

    serve_norm, (all_gate, all_up), gates = exchange_first(
        zeros, cols, weight_gate, norm_train, norm_step, (low_gate, low_up))
    weight_up, all_up = lax.optimization_barrier((weight_up, all_up))
    ups = moved(weight_up)
    serving_gate, column_gate = merge(zeros, [weight_gate, *gates], all_gate, high_gate)
    serving_up, column_up = merge(zeros, ups, all_up, high_up)
    return (serving_gate, serving_up, column_gate, column_up, serve_norm)


def solution(mesh):
    in_specs = (
        P(("job", "zero"), "cols"),
        P(("job", "zero"), None),
        P("job", "cols"),
        P(("job", "zero"), "cols"),
        P(("job", "zero"), None),
        P("job", "cols"),
        P(("job", "zero", "cols")),
        P(("job", "zero", "cols")),
    )
    out_specs = (
        P("job", "cols"),
        P("job", "cols"),
        P(("job", "cols")),
        P(("job", "cols")),
        P("job"),
    )
    return jax.shard_map(
        functools.partial(per_device, mesh.shape["zero"], mesh.shape["cols"]),
        mesh=mesh, in_specs=in_specs, out_specs=out_specs, check_vma=False
    )
```

profile of v0, /device:TPU:0, one launch (start us, length us, event | category | flops | bytes accessed | tf_op | source)
XLA Modules:
  0.0 35.8 jit_solution(18384597503846192527)
XLA Ops:
  0.6 14.5 %shard_map.119 = (bf16[16,128]{1,0:T(8,128)(2,1)}, bf16[2,1024,32]{2,1,0:T(8,128)(2,1)}, bf16[2,1024,32]{2,1,0:T(8,128)(2,1)}, bf16[1024,2048]{1,0:T(8,128)(2,1)}) custom-call(bf16[1024,2048]{1,0:T(8,128)(2,1)} %refs_0_.1, f32[2,128]{1,0:T(2,128)} %bitcast.10, f32[2,128]{1,0:T(2,128)} %bitcast.11, bf16[32,1024]{1,0:T(8,128)(2,1)} %bitcast.7, ...), custom_call_target="tpu_custom_call" | custom-call | bytes 4194304 | tf_op jit(solution)/shard_map/pallas_call | solution.py:73
  15.2 0.4 %collective-permute-start = (bf16[1024,2048]{1,0:T(8,128)(2,1)}, bf16[1024,2048]{1,0:T(8,128)(2,1)}, u32[]{:S(2)}, u32[]{:S(2)}) collective-permute-start(bf16[1024,2048]{1,0:T(8,128)(2,1)} %refs_0_.2), channel_id=1, source_target_pairs={{0,4},{4,0},{1,5},{5,1},{2,6},{6,2},{3,7},{7,3},{8,12},{12,8},{9,1... | collective-permute-start | bytes 12582920 | tf_op jit(solution)/shard_map/ppermute | solution.py:161
  15.6 9.8 %shard_map.120 = (bf16[2048,2048]{1,0:T(8,128)(2,1)}, f32[1,2048]{1,0:T(1,128)}) custom-call(bf16[1024,2048]{1,0:T(8,128)(2,1)} %refs_0_.1, bf16[1024,2048]{1,0:T(8,128)(2,1)} %get-tuple-element.15.refs_1_, bf16[2,1024,32]{2,1,0:T(8,128)(2,1)} %get-tuple-element.16.refs_2_, bf16[32,2048]{1,0:T(8,128)(2,1)} %refs_3_.2), custom_call_target="tpu_custom_call" | custom-call | flops 268435456 | bytes 16777216 | tf_op jit(solution)/shard_map/pallas_call | solution.py:134
  25.4 0.0 copy-start
  25.4 0.0 collective-permute-done.refs_1_
  25.4 9.8 %shard_map.121 = (bf16[2048,2048]{1,0:T(8,128)(2,1)}, f32[1,2048]{1,0:T(1,128)}) custom-call(bf16[1024,2048]{1,0:T(8,128)(2,1)} %refs_0_.2, bf16[1024,2048]{1,0:T(8,128)(2,1)} %collective-permute-done.refs_1_, bf16[2,1024,32]{2,1,0:T(8,128)(2,1)} %get-tuple-element.20.refs_2_, bf16[32,2048]{1,0:T(8,128)(2,1)} %refs_3_.3), custom_call_target="tpu_custom_call" | custom-call | flops 268435456 | bytes 16777216 | tf_op jit(solution)/shard_map/pallas_call | solution.py:134
  35.2 0.0 copy-done
  35.2 0.6 %copy.14 = bf16[2048]{0:T(1024)(128)(2,1)} copy(bf16[2048]{0:T(1024)(128)(2,1)S(1)} %bitcast.9) | data formatting | bytes 8192
Async XLA Ops:
  15.2 10.2 %collective-permute-start = (bf16[1024,2048]{1,0:T(8,128)(2,1)}, bf16[1024,2048]{1,0:T(8,128)(2,1)}, u32[]{:S(2)}, u32[]{:S(2)}) collective-permute-start(bf16[1024,2048]{1,0:T(8,128)(2,1)} %refs_0_.2), channel_id=1, source_target_pairs={{0,4},{4,0},{1,5},{5,1},{2,6},{6,2},{3,7},{7,3},{8,12},{12,8},{9,1... | collective-permute-start | bytes 12582920 | tf_op jit(solution)/shard_map/ppermute | solution.py:161
  25.4 9.8 %copy-start = (bf16[16,128]{1,0:T(8,128)(2,1)S(1)}, bf16[16,128]{1,0:T(8,128)(2,1)}, u32[]{:S(2)}) copy-start(bf16[16,128]{1,0:T(8,128)(2,1)} %get-tuple-element.24) | copy-start | bytes 12292
where the time goes:
time: 36 us; the launch traced here: 35.8 us
  Pallas kernels  34.1 us (95%)
  between operations  0.65 us (2%)
  local copies, waits for them, and re-layouts  0.6 us (2%)
  starting transfers between devices  0.44 us (1%)
    pallas_call x2, Pallas kernels, merge(): pl.pallas_call(functools.partial(merge_kernel, zeros, chunk), grid=(colum...  19.6 us
    pallas_call x1, Pallas kernels, exchange_first(): pl.pallas_call(functools.partial(first_kernel, zeros, cols, len(lows)), o...  14.5 us
  transfers between devices with their start and end apart: 1, of which 0 were waited for; matrix products, arithmetic and copies ran while one was open for 0% of the time, Pallas kernels for 27%

commit v1 on v0

--- a/solution.py
+++ b/solution.py
@@ -6,6 +6,7 @@
 from jax.experimental import pallas as pl
 from jax.experimental.pallas import tpu as pltpu
 from jax.sharding import PartitionSpec as P
+
 
 mix_rate = 2.0
 MESH = pl.DeviceIdType.MESH
@@ -111,6 +112,7 @@
                 low, high, preferred_element_type=jnp.float32)
             whole[s, at, :] = value
             return jnp.maximum(most, jnp.max(jnp.abs(value).reshape(chunk // 8, 8, width), axis=0))
+
         most = lax.fori_loop(0, rows // chunk, step, most, unroll=True)
     column = jnp.max(most, axis=0, keepdims=True)
     column_ref[...] = column
@@ -123,6 +125,7 @@
             out_ref[pl.ds(pl.multiple_of(base + start, chunk), chunk), :] = (
                 whole[s, pl.ds(start, chunk), :] * scale).astype(out_ref.dtype)
             return carry
+
         lax.fori_loop(0, rows // chunk, put, 0, unroll=True)
 
 
@@ -155,7 +158,7 @@
     return serving, column.reshape(columns)
 
 
-def per_device(zeros, cols, weight_gate, low_gate, high_gate, weight_up, low_up, high_up, norm_train, norm_step):
+def plain(zeros, cols, weight_gate, low_gate, high_gate, weight_up, low_up, high_up, norm_train, norm_step):
     def moved(array):
         return [array] + [
             lax.ppermute(array, "zero", [(i, (i + s) % zeros) for i in range(zeros)])
@@ -169,6 +172,273 @@
     serving_gate, column_gate = merge(zeros, [weight_gate, *gates], all_gate, high_gate)
     serving_up, column_up = merge(zeros, ups, all_up, high_up)
     return (serving_gate, serving_up, column_gate, column_up, serve_norm)
+
+
+def local_kernel(zeros, cols, width, chunk, gate_ref, up_ref, low_gate_ref, low_up_ref, high_gate_ref, high_up_ref,
+                 train_ref, step_ref, whole_gate, whole_up, column_gate, column_up, norm_ref,
+                 raw, lows, lows_t, highs, own, other, passed, mine, parts, slots,
+                 weight_sems, small_sems, norm_sems, norm_send, norm_recv, own_send, passed_recv, pass_send, other_recv,
+                 hand_send, hand_recv):
+    zero, col = lax.axis_index("zero"), lax.axis_index("cols")
+    group = zeros * cols
+    me = zero * cols + col
+    pair = col + 1 - 2 * lax.rem(col, 2)
+    top = zeros - 1
+    rows, columns = raw.shape[1:]
+    wholes = (whole_gate, whole_up)
+
+    barrier = pltpu.get_barrier_semaphore()
+    for s in range(1, cols):
+        for z in range(zeros):
+            pl.semaphore_signal(barrier, inc=1, device_id={"zero": z, "cols": lax.rem(col + s, cols)}, device_id_type=MESH)
+
+    small = []
+    for k, (low, high) in enumerate(((low_gate_ref, high_gate_ref), (low_up_ref, high_up_ref))):
+        small.append(pltpu.make_async_copy(low, lows_t.at[k], small_sems.at[k, 0]))
+        small.append(pltpu.make_async_copy(high, highs.at[k], small_sems.at[k, 1]))
+    pieces = columns // width
+    loads = [[], []]
+    for k, weight in enumerate((gate_ref, up_ref)):
+        small[2 * k].start()
+        small[2 * k + 1].start()
+        for j in range(pieces):
+            at = pl.ds(j * width, width)
+            copy = pltpu.make_async_copy(weight.at[:, at], raw.at[k, :, at], weight_sems.at[k, j])
+            copy.start()
+            loads[k].append(copy)
+    norms = [pltpu.make_async_copy(ref, parts.at[i], norm_sems.at[i]) for i, ref in enumerate((train_ref, step_ref))]
+    for copy in norms:
+        copy.start()
+
+    def column_of(k):
+        small[2 * k].wait()
+        small[2 * k + 1].wait()
+        lows[k] = lows_t[k].T
+        for j in range(pieces):
+            loads[k][j].wait()
+            at = pl.ds(j * width, width)
+            high = highs[k, :, at] * jnp.bfloat16(mix_rate)
+
+            def step(i, most):
+                here = pl.ds(pl.multiple_of(i * chunk, chunk), chunk)
+                value = raw[k, here, at].astype(jnp.float32) + jnp.dot(
+                    lows[k, here, :], high, preferred_element_type=jnp.float32)
+                wholes[k][here, at] = value
+                return jnp.maximum(most, jnp.max(jnp.abs(value).reshape(chunk // 8, 8, width), axis=0))
+
+            most = lax.fori_loop(0, rows // chunk, step, jnp.zeros((8, width), jnp.float32), unroll=True)
+            own[k, :, at] = jnp.max(most, axis=0, keepdims=True)
+
+    def send_own(k):
+        return pltpu.make_async_remote_copy(
+            src_ref=own.at[k], dst_ref=passed.at[k, zero], send_sem=own_send.at[k], recv_sem=passed_recv.at[k, zero],
+            device_id={"zero": top, "cols": pair}, device_id_type=MESH)
+
+    def take_own(k, z):
+        return pltpu.make_async_remote_copy(
+            src_ref=own.at[k], dst_ref=passed.at[k, z], send_sem=own_send.at[k], recv_sem=passed_recv.at[k, z],
+            device_id={"zero": top, "cols": pair}, device_id_type=MESH)
+
+    def pass_on(k, z):
+        return pltpu.make_async_remote_copy(
+            src_ref=passed.at[k, z], dst_ref=other.at[k], send_sem=pass_send.at[k, z], recv_sem=other_recv.at[k],
+            device_id={"zero": zeros - 1 - z, "cols": pair}, device_id_type=MESH)
+
+    def send_norm(s, z):
+        return pltpu.make_async_remote_copy(
+            src_ref=mine, dst_ref=slots.at[me], send_sem=norm_send.at[s - 1, z], recv_sem=norm_recv.at[s - 1, zero],
+            device_id={"zero": z, "cols": lax.rem(col + s, cols)}, device_id_type=MESH)
+
+    def take_norm(s, z):
+        return pltpu.make_async_remote_copy(
+            src_ref=mine, dst_ref=slots.at[z * cols + lax.rem(col - s + cols, cols)],
+            send_sem=norm_send.at[s - 1, z], recv_sem=norm_recv.at[s - 1, z],
+            device_id={"zero": z, "cols": lax.rem(col + s, cols)}, device_id_type=MESH)
+
+    def hand_on(z):
+        slot = slots.at[z * cols + pair]
+        return pltpu.make_async_remote_copy(
+            src_ref=slot, dst_ref=slot, send_sem=hand_send.at[z], recv_sem=hand_recv,
+            device_id={"zero": zeros - 1 - z, "cols": pair}, device_id_type=MESH)
+
+    column_of(0)
+    for copy in norms:
+        copy.wait()
+    mine[...] = parts[0] + parts[1]
+    pl.semaphore_wait(barrier, zeros * (cols - 1))
+    send_own(0).start()
+    for s in range(1, cols):
+        for z in range(zeros):
+            send_norm(s, z).start()
+    column_of(1)
+    send_own(1).start()
+    for s in range(1, cols):
+        for z in range(zeros):
+            take_norm(s, z).wait_recv()
+
+    @pl.when(zero == top)
+    def _():
+        for z in range(zeros):
+            take_own(0, z).wait_recv()
+            pass_on(0, z).start()
+        for z in range(zeros):
+            hand_on(z).start()
+        for z in range(zeros):
+            take_own(1, z).wait_recv()
+            pass_on(1, z).start()
+        for z in range(zeros):
+            pass_on(0, z).wait_send()
+            pass_on(1, z).wait_send()
+            hand_on(z).wait_send()
+
+    for k in range(2):
+        send_own(k).wait_send()
+    for s in range(1, cols):
+        for z in range(zeros):
+            send_norm(s, z).wait_send()
+    slots[me] = mine[...]
+    pltpu.make_async_remote_copy(
+        src_ref=mine, dst_ref=slots.at[(zeros - 1 - zero) * cols + col], send_sem=hand_send.at[0], recv_sem=hand_recv,
+        device_id={"zero": zero, "cols": pair}, device_id_type=MESH).wait_recv()
+    norm_ref[...] = jnp.concatenate([slots[g] for g in range(group)], axis=0).astype(norm_ref.dtype)
+    for k, column in enumerate((column_gate, column_up)):
+        pltpu.make_async_remote_copy(
+            src_ref=own.at[k], dst_ref=other.at[k], send_sem=own_send.at[k], recv_sem=other_recv.at[k],
+            device_id={"zero": zero, "cols": pair}, device_id_type=MESH).wait_recv()
+        column[...] = jnp.maximum(own[k], other[k])
+
+
+def local_part(zeros, cols, gate, up, low_gate, low_up, high_gate, high_up, train, step):
+    rows, columns = gate.shape
+    rank = low_gate.shape[1]
+    group = zeros * cols
+    lanes = 128 if train.shape[0] % 128 == 0 else train.shape[0]
+    tall = train.shape[0] // lanes
+    width = min(512, columns)
+    chunk = min(128, rows)
+    dma = pltpu.SemaphoreType.DMA
+    hbm, vmem = pl.BlockSpec(memory_space=pltpu.HBM), pl.BlockSpec(memory_space=pltpu.VMEM)
+    return pl.pallas_call(
+        functools.partial(local_kernel, zeros, cols, width, chunk),
+        out_shape=[pltpu.VMEM((rows, columns), jnp.float32)] * 2
+        + [pltpu.VMEM((1, columns), jnp.float32)] * 2
+        + [pltpu.VMEM((group * tall, lanes), jnp.bfloat16)],
+        in_specs=[hbm] * 8,
+        out_specs=[vmem] * 5,
+        scratch_shapes=[
+            pltpu.VMEM((2, rows, columns), gate.dtype),
+            pltpu.VMEM((2, rows, rank), gate.dtype),
+            pltpu.VMEM((2, rank, rows), gate.dtype),
+            pltpu.VMEM((2, rank, columns), gate.dtype),
+            pltpu.VMEM((2, 1, columns), jnp.float32),
+            pltpu.VMEM((2, 1, columns), jnp.float32),
+            pltpu.VMEM((2, zeros, 1, columns), jnp.float32),
+            pltpu.VMEM((tall, lanes), jnp.float32),
+            pltpu.VMEM((2, tall, lanes), jnp.float32),
+            pltpu.VMEM((group, tall, lanes), jnp.float32),
+            dma((2, columns // width)), dma((2, 2)), dma((2,)),
+            dma((cols - 1, zeros)), dma((cols - 1, zeros)),
+            dma((2,)), dma((2, zeros)), dma((2, zeros)), dma((2,)),
+            dma((zeros,)), dma,
+        ],
+        cost_estimate=pl.CostEstimate(flops=2 ** 32, bytes_accessed=2 ** 23, transcendentals=0),
+        compiler_params=pltpu.CompilerParams(collective_id=0, has_side_effects=True, vmem_limit_bytes=14 * 2 ** 20),
+    )(*[pltpu.with_memory_space_constraint(array, pltpu.HBM) for array in (
+        gate, up, low_gate.T, low_up.T, high_gate, high_up, train.reshape(tall, lanes), step.reshape(tall, lanes))])
+
+
+def write_out(value_of, chunks, chunk, stage, sems, out_ref, base, waiting):
+    slots = stage.shape[0]
+    for i in range(chunks):
+        slot = len(waiting) % slots
+        if len(waiting) >= slots:
+            waiting[-slots].wait()
+        stage[slot] = value_of(pl.ds(i * chunk, chunk)).astype(stage.dtype)
+        copy = pltpu.make_async_copy(
+            stage.at[slot], out_ref.at[pl.ds(pl.multiple_of(base + i * chunk, chunk), chunk), :], sems.at[slot])
+        copy.start()
+        waiting.append(copy)
+
+
+def remote_value(raw_ref, low_ref, high, scale):
+    def value_of(at):
+        return (raw_ref[at, :].astype(jnp.float32) + jnp.dot(
+            low_ref[at, :], high, preferred_element_type=jnp.float32)) * scale
+
+    return value_of
+
+
+def most_kernel(zeros, chunk, whole_gate, whole_up, moved, low_gate_t, low_up_t, high_ref, column_gate, column_up, norm_in,
+                gate_out, up_out, column_gate_out, column_up_out, norm_out, low_up, stage, low_gate, sems):
+    zero = lax.axis_index("zero")
+    rows = moved.shape[0]
+    column_gate_out[...] = column_gate[...]
+    column_up_out[...] = column_up[...]
+    norm_out[...] = norm_in[...]
+    high = high_ref[...] * jnp.bfloat16(mix_rate)
+    waiting = []
+    scale = 1.0 / column_gate[...]
+    chunks = rows // chunk
+    write_out(lambda at: whole_gate[at, :] * scale, chunks, chunk, stage, sems, gate_out, zero * rows, waiting)
+    low_gate[...] = low_gate_t[...].T
+    write_out(remote_value(moved, low_gate, high, scale), chunks, chunk, stage, sems, gate_out, (zeros - 1 - zero) * rows, waiting)
+    scale = 1.0 / column_up[...]
+    write_out(lambda at: whole_up[at, :] * scale, chunks, chunk, stage, sems, up_out, zero * rows, waiting)
+    low_up[...] = low_up_t[...].T
+    for copy in waiting[-stage.shape[0]:]:
+        copy.wait()
+
+
+def last_kernel(zeros, chunk, moved, low_ref, high_ref, column_ref, up_in, up_out, stage, sems):
+    zero = lax.axis_index("zero")
+    rows = moved.shape[0]
+    waiting = []
+    write_out(remote_value(moved, low_ref, high_ref[...] * jnp.bfloat16(mix_rate), 1.0 / column_ref[...]),
+              rows // chunk, chunk, stage, sems, up_out, (zeros - 1 - zero) * rows, waiting)
+    for copy in waiting[-stage.shape[0]:]:
+        copy.wait()
+
+
+def per_device(zeros, cols, weight_gate, low_gate, high_gate, weight_up, low_up, high_up, norm_train, norm_step):
+    if zeros != 2 or cols % 2:
+        return plain(zeros, cols, weight_gate, low_gate, high_gate, weight_up, low_up, high_up, norm_train, norm_step)
+    rows, columns = weight_gate.shape
+    rank = low_gate.shape[1]
+    chunk = min(128, rows)
+
+    def moved(array):
+        return lax.ppermute(array, "zero", [(i, zeros - 1 - i) for i in range(zeros)])
+
+    far_low_gate, far_low_up = moved(low_gate), moved(low_up)
+    far_gate, far_up = moved(weight_gate), moved(weight_up)
+    whole_gate, whole_up, column_gate, column_up, norm = local_part(
+        zeros, cols, weight_gate, weight_up, low_gate, low_up, high_gate, high_up, norm_train, norm_step)
+    hbm, vmem = pl.BlockSpec(memory_space=pltpu.HBM), pl.BlockSpec(memory_space=pltpu.VMEM)
+    wide = jax.ShapeDtypeStruct((rows * zeros, columns), jnp.bfloat16)
+    line = jax.ShapeDtypeStruct((1, columns), jnp.float32)
+    serving_gate, serving_up, column_gate_out, column_up_out, serve_norm, far_low = pl.pallas_call(
+        functools.partial(most_kernel, zeros, chunk),
+        out_shape=[wide, wide, line, line, jax.ShapeDtypeStruct(norm.shape, norm.dtype),
+                   pltpu.VMEM((rows, rank), low_up.dtype)],
+        in_specs=[vmem] * 9,
+        out_specs=[hbm, hbm] + [vmem] * 4,
+        scratch_shapes=[pltpu.VMEM((4, chunk, columns), jnp.bfloat16), pltpu.VMEM((rows, rank), low_gate.dtype),
+                        pltpu.SemaphoreType.DMA((4,))],
+        cost_estimate=pl.CostEstimate(flops=2 ** 32, bytes_accessed=3 * 2 ** 22, transcendentals=0),
+        compiler_params=pltpu.CompilerParams(vmem_limit_bytes=16 * 2 ** 20),
+    )(whole_gate, whole_up, far_gate, far_low_gate.T, far_low_up.T, high_gate, column_gate, column_up, norm)
+    serving_up = pl.pallas_call(
+        functools.partial(last_kernel, zeros, chunk),
+        out_shape=wide,
+        in_specs=[vmem] * 4 + [hbm],
+        out_specs=hbm,
+        input_output_aliases={4: 0},
+        scratch_shapes=[pltpu.VMEM((4, chunk, columns), jnp.bfloat16), pltpu.SemaphoreType.DMA((4,))],
+        cost_estimate=pl.CostEstimate(flops=2 ** 30, bytes_accessed=2 ** 22, transcendentals=0),
+        compiler_params=pltpu.CompilerParams(vmem_limit_bytes=16 * 2 ** 20),
+    )(far_up, far_low, high_up, column_up, serving_up)
+    return (serving_gate, serving_up, column_gate_out.reshape(columns), column_up_out.reshape(columns),
+            serve_norm.reshape(zeros * cols * norm_train.shape[0]))
 
 
 def solution(mesh):

time: 36 us -> 25.5 us (0.71)
  Pallas kernels: 34.1 us -> 23.5 us
  starting transfers between devices: 0.44 us -> 1.15 us
  local copies, waits for them, and re-layouts: 0.6 us -> 0.01 us
    pallas_call x3, Pallas kernels: 34.1 us -> 23.5 us  [the longest x1 13.3 us: local_part(): pl.pallas_call(functools.partial(local_kernel, zeros, cols, width, chunk)...]
    ppermute x1 -> x4, starting transfers between devices: 0.44 us -> 1.15 us  [moved(): lax.ppermute(array, 'zero', [(i, zeros - 1 - i) for i in range(zeros)])]
    unnamed x3 -> x4, local copies, waits for them, and re-layouts: 0.6 us -> 0.01 us
  transfers between devices with their start and end apart: 1 -> 4, of which waited for: 0 -> 0; matrix products, arithmetic and copies ran while one was open for 0% -> 0% of each run, Pallas kernels for 27% -> 81%
where the time goes in v1:
time: 25.5 us; the launch traced here: 25.3 us
  Pallas kernels  23.5 us (92%)
  starting transfers between devices  1.15 us (5%)
  between operations  0.71 us (3%)
    pallas_call x1, Pallas kernels, local_part(): pl.pallas_call(functools.partial(local_kernel, zeros, cols, width, chunk)...  13.3 us
    pallas_call x1, Pallas kernels, per_device(): pl.pallas_call(functools.partial(most_kernel, zeros, chunk), out_shape=[w...  7.16 us
    pallas_call x1, Pallas kernels, per_device(): pl.pallas_call(functools.partial(last_kernel, zeros, chunk), out_shape=wi...  2.99 us
    ppermute x4, starting transfers between devices, moved(): lax.ppermute(array, 'zero', [(i, zeros - 1 - i) for i in range(zeros)])  1.15 us
  transfers between devices with their start and end apart: 4, of which 0 were waited for; matrix products, arithmetic and copies ran while one was open for 0% of the time, Pallas kernels for 81%

profile of v1, /device:TPU:0, one launch (start us, length us, event | category | flops | bytes accessed | tf_op | source)
XLA Modules:
  0.0 25.3 jit_solution(2193143921925298036)
XLA Ops:
  0.6 0.0 copy-start
  0.6 0.6 %collective-permute-start = (bf16[1024,2048]{1,0:T(8,128)(2,1)}, bf16[1024,2048]{1,0:T(8,128)(2,1)S(1)}, u32[]{:S(2)}, u32[]{:S(2)}) collective-permute-start(bf16[1024,2048]{1,0:T(8,128)(2,1)} %gate_ref.1), channel_id=1, source_target_pairs={{0,4},{4,0},{1,5},{5,1},{2,6},{6,2},{3,7},{7,3},{8,12},{12,8},{9,1... | collective-permute-start | bytes 12582920 | tf_op jit(solution)/shard_map/ppermute | solution.py:410
  1.2 0.1 collective-permute-start.3
  1.3 0.4 %collective-permute-start.1 = (bf16[1024,32]{0,1:T(8,128)(2,1)}, bf16[1024,32]{0,1:T(8,128)(2,1)S(1)}, u32[]{:S(2)}, u32[]{:S(2)}) collective-permute-start(bf16[1024,32]{0,1:T(8,128)(2,1)} %param.9), channel_id=1, source_target_pairs={{0,4},{4,0},{1,5},{5,1},{2,6},{6,2},{3,7},{7,3},{8,12},{12,8},{9,1... | collective-permute-start | bytes 196616 | tf_op jit(solution)/shard_map/ppermute | solution.py:410
  1.7 0.1 collective-permute-start.2
  1.8 13.3 %shard_map.119 = (f32[1024,2048]{1,0:T(8,128)S(1)}, f32[1024,2048]{1,0:T(8,128)S(1)}, f32[1,2048]{1,0:T(1,128)S(1)}, f32[1,2048]{1,0:T(1,128)S(1)}, bf16[16,128]{1,0:T(8,128)(2,1)S(1)}) custom-call(bf16[1024,2048]{1,0:T(8,128)(2,1)} %gate_ref.1, bf16[1024,2048]{1,0:T(8,128)(2,1)} %up_ref.1, bf16[32,1024]{1,0:T(8,128)(2,1)} %bitcast.11, ...), custom_call_target="tpu_custom_call" | custom-call | flops 4294967296 | bytes 8388608 | tf_op jit(solution)/shard_map/pallas_call | solution.py:321
  15.1 0.0 collective-permute-done.1
  15.1 0.0 collective-permute-done.2
  15.1 0.0 collective-permute-done.moved
  15.1 0.0 copy-done
  15.1 0.0 copy-start.1
  15.2 7.2 %shard_map.120 = (bf16[2048,2048]{1,0:T(8,128)(2,1)}, bf16[2048,2048]{1,0:T(8,128)(2,1)}, f32[1,2048]{1,0:T(1,128)}, f32[1,2048]{1,0:T(1,128)}, bf16[16,128]{1,0:T(8,128)(2,1)}, /*index=5*/bf16[1024,32]{1,0:T(8,128)(2,1)S(1)}) custom-call(f32[1024,2048]{1,0:T(8,128)S(1)} %get-tuple-element.16.whole_gate, f32[1024,2048]{1,0:T(8,128)S(1)} %get-tuple-element.17.whole_up, ...), custom_call_target="tpu_custom_call" | custom-call | flops 4294967296 | bytes 12582912 | tf_op jit(solution)/shard_map/pallas_call | solution.py:419
  22.3 0.0 collective-permute-done.3.moved
  22.3 0.0 copy-done.1
  22.4 3.0 %shard_map.121 = bf16[2048,2048]{1,0:T(8,128)(2,1)} custom-call(bf16[1024,2048]{1,0:T(8,128)(2,1)S(1)} %collective-permute-done.3.moved, bf16[1024,32]{1,0:T(8,128)(2,1)S(1)} %get-tuple-element.22.low_ref, bf16[32,2048]{1,0:T(8,128)(2,1)S(1)} %copy-done.1, f32[1,2048]{1,0:T(1,128)S(1)} %get-tuple-element.19.column_up.column_ref, ...), custom_call_target="tpu_custom_call", output_to_operand_aliasing={{}: (4, {})} | custom-call | flops 1073741824 | bytes 4194304 | tf_op jit(solution)/shard_map/pallas_call | solution.py:430
Async XLA Ops:
  0.6 14.5 %copy-start = (bf16[32,2048]{1,0:T(8,128)(2,1)S(1)}, bf16[32,2048]{1,0:T(8,128)(2,1)}, u32[]{:S(2)}) copy-start(bf16[32,2048]{1,0:T(8,128)(2,1)} %high_ref.2) | copy-start | bytes 393220
  0.6 14.5 %collective-permute-start = (bf16[1024,2048]{1,0:T(8,128)(2,1)}, bf16[1024,2048]{1,0:T(8,128)(2,1)S(1)}, u32[]{:S(2)}, u32[]{:S(2)}) collective-permute-start(bf16[1024,2048]{1,0:T(8,128)(2,1)} %gate_ref.1), channel_id=1, source_target_pairs={{0,4},{4,0},{1,5},{5,1},{2,6},{6,2},{3,7},{7,3},{8,12},{12,8},{9,1... | collective-permute-start | bytes 12582920 | tf_op jit(solution)/shard_map/ppermute | solution.py:410
  1.2 21.1 %collective-permute-start.3 = (bf16[1024,2048]{1,0:T(8,128)(2,1)}, bf16[1024,2048]{1,0:T(8,128)(2,1)S(1)}, u32[]{:S(2)}, u32[]{:S(2)}) collective-permute-start(bf16[1024,2048]{1,0:T(8,128)(2,1)} %up_ref.1), channel_id=1, source_target_pairs={{0,4},{4,0},{1,5},{5,1},{2,6},{6,2},{3,7},{7,3},{8,12},{12,8},{9,1... | collective-permute-start | bytes 12582920 | tf_op jit(solution)/shard_map/ppermute | solution.py:410
  1.3 13.8 %collective-permute-start.1 = (bf16[1024,32]{0,1:T(8,128)(2,1)}, bf16[1024,32]{0,1:T(8,128)(2,1)S(1)}, u32[]{:S(2)}, u32[]{:S(2)}) collective-permute-start(bf16[1024,32]{0,1:T(8,128)(2,1)} %param.9), channel_id=1, source_target_pairs={{0,4},{4,0},{1,5},{5,1},{2,6},{6,2},{3,7},{7,3},{8,12},{12,8},{9,1... | collective-permute-start | bytes 196616 | tf_op jit(solution)/shard_map/ppermute | solution.py:410
  1.7 13.4 %collective-permute-start.2 = (bf16[1024,32]{0,1:T(8,128)(2,1)}, bf16[1024,32]{0,1:T(8,128)(2,1)S(1)}, u32[]{:S(2)}, u32[]{:S(2)}) collective-permute-start(bf16[1024,32]{0,1:T(8,128)(2,1)} %param.12), channel_id=1, source_target_pairs={{0,4},{4,0},{1,5},{5,1},{2,6},{6,2},{3,7},{7,3},{8,12},{12,8},{9,1... | collective-permute-start | bytes 196616 | tf_op jit(solution)/shard_map/ppermute | solution.py:410
  15.1 7.2 %copy-start.1 = (bf16[32,2048]{1,0:T(8,128)(2,1)S(1)}, bf16[32,2048]{1,0:T(8,128)(2,1)}, u32[]{:S(2)}) copy-start(bf16[32,2048]{1,0:T(8,128)(2,1)} %high_ref.3) | copy-start | bytes 393220

commit v2 on v0

--- a/solution.py
+++ b/solution.py
@@ -6,6 +6,7 @@
 from jax.experimental import pallas as pl
 from jax.experimental.pallas import tpu as pltpu
 from jax.sharding import PartitionSpec as P
+
 
 mix_rate = 2.0
 MESH = pl.DeviceIdType.MESH
@@ -111,6 +112,7 @@
                 low, high, preferred_element_type=jnp.float32)
             whole[s, at, :] = value
             return jnp.maximum(most, jnp.max(jnp.abs(value).reshape(chunk // 8, 8, width), axis=0))
+
         most = lax.fori_loop(0, rows // chunk, step, most, unroll=True)
     column = jnp.max(most, axis=0, keepdims=True)
     column_ref[...] = column
@@ -123,6 +125,7 @@
             out_ref[pl.ds(pl.multiple_of(base + start, chunk), chunk), :] = (
                 whole[s, pl.ds(start, chunk), :] * scale).astype(out_ref.dtype)
             return carry
+
         lax.fori_loop(0, rows // chunk, put, 0, unroll=True)
 
 
@@ -155,7 +158,7 @@
     return serving, column.reshape(columns)
 
 
-def per_device(zeros, cols, weight_gate, low_gate, high_gate, weight_up, low_up, high_up, norm_train, norm_step):
+def plain(zeros, cols, weight_gate, low_gate, high_gate, weight_up, low_up, high_up, norm_train, norm_step):
     def moved(array):
         return [array] + [
             lax.ppermute(array, "zero", [(i, (i + s) % zeros) for i in range(zeros)])
@@ -169,6 +172,237 @@
     serving_gate, column_gate = merge(zeros, [weight_gate, *gates], all_gate, high_gate)
     serving_up, column_up = merge(zeros, ups, all_up, high_up)
     return (serving_gate, serving_up, column_gate, column_up, serve_norm)
+
+
+def local_kernel(zeros, cols, width, chunk, gate_ref, up_ref, low_gate_ref, low_up_ref, high_gate_ref, high_up_ref,
+                 train_ref, step_ref, whole_gate, whole_up, up_first, up_second, far_lows, most, far_most, norm_ref,
+                 raw, lows, lows_t, highs, parts, weight_sems, small_sems, norm_sems, norm_send, norm_recv,
+                 near_send, near_recv):
+    zero, col = lax.axis_index("zero"), lax.axis_index("cols")
+    me = zero * cols + col
+    rows, columns = raw.shape
+    pieces = columns // width
+    split = up_first.shape[0]
+    ahead = 3
+
+    barrier = pltpu.get_barrier_semaphore()
+    for z in range(1, zeros):
+        pl.semaphore_signal(barrier, inc=1, device_id={"zero": lax.rem(zero + z, zeros), "cols": col}, device_id_type=MESH)
+    for s in range(1, cols):
+        for z in range(zeros):
+            pl.semaphore_signal(barrier, inc=1, device_id={"zero": z, "cols": lax.rem(col + s, cols)}, device_id_type=MESH)
+
+    loads = []
+    for j in range(pieces):
+        at = pl.ds(j * width, width)
+        loads.append([pltpu.make_async_copy(gate_ref.at[:, at], raw.at[:, at], weight_sems.at[0, j])])
+    for j in range(pieces):
+        at = pl.ds(j * width, width)
+        loads.append([pltpu.make_async_copy(up_ref.at[pl.ds(0, split), at], up_first.at[:, at], weight_sems.at[1, j]),
+                      pltpu.make_async_copy(up_ref.at[pl.ds(split, rows - split), at], up_second.at[:, at], weight_sems.at[2, j])])
+    small = []
+    for k, (low, high) in enumerate(((low_gate_ref, high_gate_ref), (low_up_ref, high_up_ref))):
+        small.append(pltpu.make_async_copy(low, lows_t.at[k], small_sems.at[k, 0]))
+        small.append(pltpu.make_async_copy(high, highs.at[k], small_sems.at[k, 1]))
+    norms = [pltpu.make_async_copy(ref, parts.at[i], norm_sems.at[i]) for i, ref in enumerate((train_ref, step_ref))]
+    for copy in norms + small[:2] + sum(loads[:ahead], []) + small[2:]:
+        copy.start()
+
+    def norm_copy(i, s, z, rank, recv):
+        return pltpu.make_async_remote_copy(
+            src_ref=(train_ref, step_ref)[i], dst_ref=norm_ref.at[i, rank],
+            send_sem=norm_send.at[i, s - 1, z], recv_sem=norm_recv.at[i, s - 1, recv],
+            device_id={"zero": z, "cols": lax.rem(col + s, cols)}, device_id_type=MESH)
+
+    def near_copy(i, src, dst):
+        return pltpu.make_async_remote_copy(
+            src_ref=src, dst_ref=dst, send_sem=near_send.at[i], recv_sem=near_recv.at[i],
+            device_id={"zero": zeros - 1 - zero, "cols": col}, device_id_type=MESH)
+
+    def near_copies(rank):
+        return [near_copy(0, low_gate_ref, far_lows.at[0]), near_copy(1, low_up_ref, far_lows.at[1]),
+                near_copy(2, train_ref, norm_ref.at[0, rank]), near_copy(3, step_ref, norm_ref.at[1, rank])]
+
+    peers = [(i, s, z) for s in range(cols - 1, 0, -1) for z in range(zeros) for i in range(2)]
+    entry = jnp.maximum(2 * pieces * (cols - 1 - col) // cols - 1, 0)
+    for n in range(2 * pieces):
+        @pl.when(entry == n)
+        def _():
+            pl.semaphore_wait(barrier, zeros * cols - 1)
+            for i, s, z in peers:
+                norm_copy(i, s, z, me, zero).start()
+            for copy in near_copies(me):
+                copy.start()
+
+        k, j = n // pieces, n % pieces
+        if j == 0:
+            small[2 * k].wait()
+            small[2 * k + 1].wait()
+            lows[k] = lows_t[k].T
+        for copy in loads[n]:
+            copy.wait()
+        if n + ahead < len(loads):
+            for copy in loads[n + ahead]:
+                copy.start()
+        at = pl.ds(j * width, width)
+        high = highs[k, :, at] * jnp.bfloat16(mix_rate)
+        whole = (whole_gate, whole_up)[k]
+        value_most = jnp.zeros((8, width), jnp.float32)
+        for i in range(rows // chunk):
+            here = pl.ds(i * chunk, chunk)
+            if k == 0:
+                part = raw[here, at]
+            elif i * chunk < split:
+                part = up_first[here, at]
+            else:
+                part = up_second[pl.ds(i * chunk - split, chunk), at]
+            value = part.astype(jnp.float32) + jnp.dot(lows[k, here, :], high, preferred_element_type=jnp.float32)
+            whole[here, at] = value
+            value_most = jnp.maximum(value_most, jnp.max(jnp.abs(value).reshape(chunk // 8, 8, width), axis=0))
+        most[:, pl.ds(k * columns + j * width, width)] = jnp.max(value_most, axis=0, keepdims=True)
+    give = near_copy(4, most, far_most)
+    give.start()
+    for copy in norms:
+        copy.wait()
+    for i in range(2):
+        norm_ref[i, me] = parts[i]
+    for i, s, z in peers:
+        norm_copy(i, s, z, me, zero).wait_send()
+        norm_copy(i, s, z, z * cols + lax.rem(col - s + cols, cols), z).wait_recv()
+    for copy in near_copies(me):
+        copy.wait_send()
+    for copy in near_copies((zeros - 1 - zero) * cols + col):
+        copy.wait_recv()
+    give.wait()
+
+
+def local_part(zeros, cols, split, gate, up, low_gate, low_up, high_gate, high_up, train, step):
+    rows, columns = gate.shape
+    rank = low_gate.shape[1]
+    group = zeros * cols
+    lanes = 128 if train.shape[0] % 128 == 0 else train.shape[0]
+    tall = train.shape[0] // lanes
+    width = min(512, columns)
+    chunk = min(128, rows)
+    dma = pltpu.SemaphoreType.DMA
+    hbm, vmem = pl.BlockSpec(memory_space=pltpu.HBM), pl.BlockSpec(memory_space=pltpu.VMEM)
+    return pl.pallas_call(
+        functools.partial(local_kernel, zeros, cols, width, chunk),
+        out_shape=[pltpu.VMEM((rows, columns), jnp.float32)] * 2
+        + [pltpu.VMEM((split, columns), up.dtype), pltpu.VMEM((rows - split, columns), up.dtype),
+           pltpu.VMEM((2, rank, rows), gate.dtype)]
+        + [pltpu.VMEM((1, 2 * columns), jnp.float32)] * 2
+        + [pltpu.VMEM((2, group, tall, lanes), jnp.float32)],
+        in_specs=[hbm] * 8,
+        out_specs=[vmem] * 8,
+        scratch_shapes=[
+            pltpu.VMEM((rows, columns), gate.dtype),
+            pltpu.VMEM((2, rows, rank), gate.dtype),
+            pltpu.VMEM((2, rank, rows), gate.dtype),
+            pltpu.VMEM((2, rank, columns), gate.dtype),
+            pltpu.VMEM((2, tall, lanes), jnp.float32),
+            dma((3, columns // width)), dma((2, 2)), dma((2,)),
+            dma((2, cols - 1, zeros)), dma((2, cols - 1, zeros)), dma((5,)), dma((5,)),
+        ],
+        cost_estimate=pl.CostEstimate(flops=2 ** 32, bytes_accessed=2 ** 23, transcendentals=0),
+        compiler_params=pltpu.CompilerParams(collective_id=0, has_side_effects=True, vmem_limit_bytes=10 * 2 ** 20),
+    )(*[pltpu.with_memory_space_constraint(array, pltpu.HBM) for array in (
+        gate, up, low_gate.T, low_up.T, high_gate, high_up, train.reshape(tall, lanes), step.reshape(tall, lanes))])
+
+
+def write_rows(value_of, chunk, stage, out_ref, base, sems):
+    copies = []
+    for i in range(stage.shape[0] // chunk):
+        here = pl.ds(i * chunk, chunk)
+        stage[here, :] = value_of(here).astype(stage.dtype)
+        copies.append(pltpu.make_async_copy(
+            stage.at[here, :], out_ref.at[pl.ds(pl.multiple_of(base + i * chunk, chunk), chunk), :], sems.at[i]))
+        copies[-1].start()
+    return copies
+
+
+def far_value(moved, low_ref, first, high, scale):
+    return lambda here: (moved[here, :].astype(jnp.float32) + jnp.dot(
+        low_ref[pl.ds(first + here.start, here.size), :], high, preferred_element_type=jnp.float32)) * scale
+
+
+def most_kernel(zeros, cols, chunk, whole_gate, whole_up, moved, far_lows, high_ref, most, far_most, norm_in,
+                gate_out, up_out, column_gate_out, column_up_out, norm_out, low_up, column_up,
+                stage, low_gate, column_gate, norm, sems, line_sems):
+    zero = lax.axis_index("zero")
+    rows, columns = moved.shape
+    near, far = zero * rows, (zeros - 1 - zero) * rows
+    for k, column in enumerate((column_gate, column_up)):
+        at = pl.ds(k * columns, columns)
+        column[...] = jnp.maximum(most[:, at], far_most[:, at])
+    scale = 1.0 / column_up[...]
+    copies = write_rows(lambda here: whole_up[here, :] * scale, chunk, stage.at[0], up_out, near, sems.at[0])
+    gate_scale = 1.0 / column_gate[...]
+    copies += write_rows(lambda here: whole_gate[here, :] * gate_scale, chunk, stage.at[1], gate_out, near, sems.at[1])
+    norm[...] = jnp.concatenate([norm_in[0, g] + norm_in[1, g] for g in range(zeros * cols)], axis=0).astype(norm.dtype)
+    for i, (src, dst) in enumerate(((column_gate, column_gate_out), (column_up, column_up_out), (norm, norm_out))):
+        copies.append(pltpu.make_async_copy(src, dst, line_sems.at[i]))
+        copies[-1].start()
+    low_gate[...] = far_lows[0].T
+    high = high_ref[...] * jnp.bfloat16(mix_rate)
+    copies += write_rows(far_value(moved, low_gate, 0, high, gate_scale), chunk, stage.at[2], gate_out, far, sems.at[2])
+    low_up[...] = far_lows[1].T
+    for copy in copies:
+        copy.wait()
+
+
+def last_kernel(zeros, chunk, rows, first, moved, low_ref, high_ref, column_ref, up_in, up_out, stage, sems):
+    zero = lax.axis_index("zero")
+    high, scale = high_ref[...] * jnp.bfloat16(mix_rate), 1.0 / column_ref[...]
+    for copy in write_rows(far_value(moved, low_ref, first, high, scale), chunk, stage, up_out,
+                           (zeros - 1 - zero) * rows + first, sems):
+        copy.wait()
+
+
+def per_device(zeros, cols, weight_gate, low_gate, high_gate, weight_up, low_up, high_up, norm_train, norm_step):
+    rows, columns = weight_gate.shape
+    rank = low_gate.shape[1]
+    chunk = min(128, rows)
+    split = rows * 3 // 4 // chunk * chunk
+    if zeros != 2 or not split:
+        return plain(zeros, cols, weight_gate, low_gate, high_gate, weight_up, low_up, high_up, norm_train, norm_step)
+
+    def moved(array):
+        return lax.ppermute(array, "zero", [(i, zeros - 1 - i) for i in range(zeros)])
+
+    far_gate = moved(weight_gate)
+    whole_gate, whole_up, up_first, up_second, far_lows, most, far_most, norm = local_part(
+        zeros, cols, split, weight_gate, weight_up, low_gate, low_up, high_gate, high_up, norm_train, norm_step)
+    far_up = [moved(up_first), moved(up_second)]
+    hbm, vmem = pl.BlockSpec(memory_space=pltpu.HBM), pl.BlockSpec(memory_space=pltpu.VMEM)
+    wide = jax.ShapeDtypeStruct((rows * zeros, columns), jnp.bfloat16)
+    line = jax.ShapeDtypeStruct((1, columns), jnp.float32)
+    group, tall, lanes = norm.shape[1:]
+    serving_gate, serving_up, column_gate, column_up, serve_norm, far_low, up_line = pl.pallas_call(
+        functools.partial(most_kernel, zeros, cols, chunk),
+        out_shape=[wide, wide, line, line, jax.ShapeDtypeStruct((group * tall, lanes), jnp.bfloat16),
+                   pltpu.VMEM((rows, rank), low_up.dtype), pltpu.VMEM((1, columns), jnp.float32)],
+        in_specs=[vmem] * 8,
+        out_specs=[hbm] * 5 + [vmem] * 2,
+        scratch_shapes=[pltpu.VMEM((3, rows, columns), jnp.bfloat16), pltpu.VMEM((rows, rank), low_gate.dtype),
+                        pltpu.VMEM((1, columns), jnp.float32), pltpu.VMEM((group * tall, lanes), jnp.bfloat16),
+                        pltpu.SemaphoreType.DMA((3, rows // chunk)), pltpu.SemaphoreType.DMA((3,))],
+        cost_estimate=pl.CostEstimate(flops=2 ** 32, bytes_accessed=3 * 2 ** 22, transcendentals=0),
+        compiler_params=pltpu.CompilerParams(vmem_limit_bytes=16 * 2 ** 20),
+    )(whole_gate, whole_up, far_gate, far_lows, high_gate, most, far_most, norm)
+    for far, first in zip(far_up, (0, split)):
+        serving_up = pl.pallas_call(
+            functools.partial(last_kernel, zeros, chunk, rows, first),
+            out_shape=wide,
+            in_specs=[vmem] * 4 + [hbm],
+            out_specs=hbm,
+            input_output_aliases={4: 0},
+            scratch_shapes=[pltpu.VMEM(far.shape, jnp.bfloat16), pltpu.SemaphoreType.DMA((far.shape[0] // chunk,))],
+            cost_estimate=pl.CostEstimate(flops=2 ** 30, bytes_accessed=2 ** 22, transcendentals=0),
+            compiler_params=pltpu.CompilerParams(vmem_limit_bytes=16 * 2 ** 20),
+        )(far, far_low, high_up, up_line, serving_up)
+    return (serving_gate, serving_up, column_gate.reshape(columns), column_up.reshape(columns),
+            serve_norm.reshape(group * tall * lanes))
 
 
 def solution(mesh):

time: 36 us -> 18.2 us (0.51)
  Pallas kernels: 34.1 us -> 16.1 us
  starting transfers between devices: 0.44 us -> 1.13 us
  local copies, waits for them, and re-layouts: 0.6 us -> 0.01 us
    pallas_call x3 -> x4, Pallas kernels: 34.1 us -> 16.1 us  [the longest x1 7.82 us: local_part(): pl.pallas_call(functools.partial(local_kernel, zeros, cols, width, chunk)...]
    ppermute x1 -> x3, starting transfers between devices: 0.44 us -> 1.13 us  [moved(): lax.ppermute(array, 'zero', [(i, zeros - 1 - i) for i in range(zeros)])]
    unnamed x3 -> x4, local copies, waits for them, and re-layouts: 0.6 us -> 0.01 us
  transfers between devices with their start and end apart: 1 -> 3, of which waited for: 0 -> 1; matrix products, arithmetic and copies ran while one was open for 0% -> 0% of each run, Pallas kernels for 27% -> 82%
where the time goes in v2:
time: 18.2 us; the launch traced here: 18 us
  Pallas kernels  16.1 us (88%)
  starting transfers between devices  1.13 us (6%)
  between operations  0.68 us (4%)
    pallas_call x1, Pallas kernels, local_part(): pl.pallas_call(functools.partial(local_kernel, zeros, cols, width, chunk)...  7.82 us
    pallas_call x1, Pallas kernels, per_device(): pl.pallas_call(functools.partial(most_kernel, zeros, cols, chunk), out_sh...  5.01 us
    pallas_call x2, Pallas kernels, per_device(): pl.pallas_call(functools.partial(last_kernel, zeros, chunk, rows, first),...  3.24 us
    ppermute x3, starting transfers between devices, moved(): lax.ppermute(array, 'zero', [(i, zeros - 1 - i) for i in range(zeros)])  1.13 us
  transfers between devices with their start and end apart: 3, of which 1 were waited for; matrix products, arithmetic and copies ran while one was open for 0% of the time, Pallas kernels for 82%

profile of v2, /device:TPU:0, one launch (start us, length us, event | category | flops | bytes accessed | tf_op | source)
XLA Modules:
  0.0 18.0 jit_solution(4143914808756187146)
XLA Ops:
  0.6 0.0 copy-start.1
  0.6 0.6 %collective-permute-start = (bf16[1024,2048]{1,0:T(8,128)(2,1)}, bf16[1024,2048]{1,0:T(8,128)(2,1)S(1)}, u32[]{:S(2)}, u32[]{:S(2)}) collective-permute-start(bf16[1024,2048]{1,0:T(8,128)(2,1)} %gate_ref.1), channel_id=1, source_target_pairs={{0,4},{4,0},{1,5},{5,1},{2,6},{6,2},{3,7},{7,3},{8,12},{12,8},{9,1... | collective-permute-start | bytes 12582920 | tf_op jit(solution)/shard_map/ppermute | solution.py:371
  1.2 7.8 %shard_map.119 = (f32[1024,2048]{1,0:T(8,128)S(1)}, f32[1024,2048]{1,0:T(8,128)S(1)}, bf16[768,2048]{1,0:T(8,128)(2,1)S(1)}, bf16[256,2048]{1,0:T(8,128)(2,1)S(1...) custom-call(bf16[1024,2048]{1,0:T(8,128)(2,1)} %gate_ref.1, ...), custom_call_target="tpu_custom_call" | custom-call | flops 4294967296 | bytes 8388608 | tf_op jit(solution)/shard_map/pallas_call | solution.py:289
  9.0 0.3 %collective-permute-start.2 = (bf16[768,2048]{1,0:T(8,128)(2,1)S(1)}, bf16[768,2048]{1,0:T(8,128)(2,1)S(1)}, u32[]{:S(2)}, u32[]{:S(2)}) collective-permute-start(bf16[768,2048]{1,0:T(8,128)(2,1)S(1)} %get-tuple-element.30), channel_id=1, source_target_pairs={{0,4},{4,0},{1,5},{5,1},{2,6},{6,2},{3,7},{7,3},{8,12},{12,8},{9,1... | collective-permute-start | bytes 9437192 | tf_op jit(solution)/shard_map/ppermute | solution.py:371
  9.3 0.3 %collective-permute-start.1 = (bf16[256,2048]{1,0:T(8,128)(2,1)S(1)}, bf16[256,2048]{1,0:T(8,128)(2,1)S(1)}, u32[]{:S(2)}, u32[]{:S(2)}) collective-permute-start(bf16[256,2048]{1,0:T(8,128)(2,1)S(1)} %get-tuple-element.27), channel_id=1, source_target_pairs={{0,4},{4,0},{1,5},{5,1},{2,6},{6,2},{3,7},{7,3},{8,12},{12,8},{9,1... | collective-permute-start | bytes 3145736 | tf_op jit(solution)/shard_map/ppermute | solution.py:371
  9.6 0.0 collective-permute-done.moved
  9.6 0.0 copy-done.1
  9.6 0.0 copy-start
  9.6 5.0 %shard_map.120 = (bf16[2048,2048]{1,0:T(8,128)(2,1)}, bf16[2048,2048]{1,0:T(8,128)(2,1)}, f32[1,2048]{1,0:T(1,128)}, f32[1,2048]{1,0:T(1,128)}, bf16[16,128]{1,0...) custom-call(f32[1024,2048]{1,0:T(8,128)S(1)} %get-tuple-element.20.whole_gate, ...), custom_call_target="tpu_custom_call" | custom-call | flops 4294967296 | bytes 12582912 | tf_op jit(solution)/shard_map/pallas_call | solution.py:381
  14.6 0.1 collective-permute-done.2.moved
  14.8 0.0 copy-done
  14.8 2.0 %shard_map.121.up_in = bf16[2048,2048]{1,0:T(8,128)(2,1)} custom-call(bf16[768,2048]{1,0:T(8,128)(2,1)S(1)} %collective-permute-done.2.moved, bf16[1024,32]{1,0:T(8,128)(2,1)S(1)} %get-tuple-element.28.low_ref, bf16[32,2048]{1,0:T(8,128)(2,1)S(1)} %copy-done, f32[1,2048]{1,0:T(1,128)S(1)} %get-tuple-element.29.column_ref, ...), custom_call_target="tpu_custom_call", output_to_operand_aliasing={{}: (4, {})} | custom-call | flops 1073741824 | bytes 4194304 | tf_op jit(solution)/shard_map/pallas_call | solution.py:394
  16.7 0.0 collective-permute-done.1.moved
  16.8 1.3 %shard_map.122 = bf16[2048,2048]{1,0:T(8,128)(2,1)} custom-call(bf16[256,2048]{1,0:T(8,128)(2,1)S(1)} %collective-permute-done.1.moved, bf16[1024,32]{1,0:T(8,128)(2,1)S(1)} %get-tuple-element.28.low_ref, bf16[32,2048]{1,0:T(8,128)(2,1)S(1)} %copy-done, f32[1,2048]{1,0:T(1,128)S(1)} %get-tuple-element.29.column_ref, ...), custom_call_target="tpu_custom_call", output_to_operand_aliasing={{}: (4, {})} | custom-call | flops 1073741824 | bytes 4194304 | tf_op jit(solution)/shard_map/pallas_call | solution.py:394
Async XLA Ops:
  0.6 9.0 %copy-start.1 = (bf16[32,2048]{1,0:T(8,128)(2,1)S(1)}, bf16[32,2048]{1,0:T(8,128)(2,1)}, u32[]{:S(2)}) copy-start(bf16[32,2048]{1,0:T(8,128)(2,1)} %high_ref.3) | copy-start | bytes 393220
  0.6 9.0 %collective-permute-start = (bf16[1024,2048]{1,0:T(8,128)(2,1)}, bf16[1024,2048]{1,0:T(8,128)(2,1)S(1)}, u32[]{:S(2)}, u32[]{:S(2)}) collective-permute-start(bf16[1024,2048]{1,0:T(8,128)(2,1)} %gate_ref.1), channel_id=1, source_target_pairs={{0,4},{4,0},{1,5},{5,1},{2,6},{6,2},{3,7},{7,3},{8,12},{12,8},{9,1... | collective-permute-start | bytes 12582920 | tf_op jit(solution)/shard_map/ppermute | solution.py:371
  9.0 5.7 %collective-permute-start.2 = (bf16[768,2048]{1,0:T(8,128)(2,1)S(1)}, bf16[768,2048]{1,0:T(8,128)(2,1)S(1)}, u32[]{:S(2)}, u32[]{:S(2)}) collective-permute-start(bf16[768,2048]{1,0:T(8,128)(2,1)S(1)} %get-tuple-element.30), channel_id=1, source_target_pairs={{0,4},{4,0},{1,5},{5,1},{2,6},{6,2},{3,7},{7,3},{8,12},{12,8},{9,1... | collective-permute-start | bytes 9437192 | tf_op jit(solution)/shard_map/ppermute | solution.py:371
  9.3 7.4 %collective-permute-start.1 = (bf16[256,2048]{1,0:T(8,128)(2,1)S(1)}, bf16[256,2048]{1,0:T(8,128)(2,1)S(1)}, u32[]{:S(2)}, u32[]{:S(2)}) collective-permute-start(bf16[256,2048]{1,0:T(8,128)(2,1)S(1)} %get-tuple-element.27), channel_id=1, source_target_pairs={{0,4},{4,0},{1,5},{5,1},{2,6},{6,2},{3,7},{7,3},{8,12},{12,8},{9,1... | collective-permute-start | bytes 3145736 | tf_op jit(solution)/shard_map/ppermute | solution.py:371
  9.6 5.1 %copy-start = (bf16[32,2048]{1,0:T(8,128)(2,1)S(1)}, bf16[32,2048]{1,0:T(8,128)(2,1)}, u32[]{:S(2)}) copy-start(bf16[32,2048]{1,0:T(8,128)(2,1)} %high_ref.5) | copy-start | bytes 393220

commit v3 on v2

--- a/solution.py
+++ b/solution.py
@@ -363,7 +363,7 @@
     rows, columns = weight_gate.shape
     rank = low_gate.shape[1]
     chunk = min(128, rows)
-    split = rows * 3 // 4 // chunk * chunk
+    split = rows * 5 // 8 // chunk * chunk
     if zeros != 2 or not split:
         return plain(zeros, cols, weight_gate, low_gate, high_gate, weight_up, low_up, high_up, norm_train, norm_step)
 
@@ -392,12 +392,12 @@
     )(whole_gate, whole_up, far_gate, far_lows, high_gate, most, far_most, norm)
     for far, first in zip(far_up, (0, split)):
         serving_up = pl.pallas_call(
-            functools.partial(last_kernel, zeros, chunk, rows, first),
+            functools.partial(last_kernel, zeros, chunk // 2, rows, first),
             out_shape=wide,
             in_specs=[vmem] * 4 + [hbm],
             out_specs=hbm,
             input_output_aliases={4: 0},
-            scratch_shapes=[pltpu.VMEM(far.shape, jnp.bfloat16), pltpu.SemaphoreType.DMA((far.shape[0] // chunk,))],
+            scratch_shapes=[pltpu.VMEM(far.shape, jnp.bfloat16), pltpu.SemaphoreType.DMA((far.shape[0] * 2 // chunk,))],
             cost_estimate=pl.CostEstimate(flops=2 ** 30, bytes_accessed=2 ** 22, transcendentals=0),
             compiler_params=pltpu.CompilerParams(vmem_limit_bytes=16 * 2 ** 20),
         )(far, far_low, high_up, up_line, serving_up)

time: 18.2 us -> 18 us (0.989)
  transfers between devices with their start and end apart: 3 -> 3, of which waited for: 1 -> 0; matrix products, arithmetic and copies ran while one was open for 0% -> 0% of each run, Pallas kernels for 82% -> 82%
where the time goes in v3:
time: 18 us; the launch traced here: 17.9 us
  Pallas kernels  16 us (89%)
  starting transfers between devices  1.13 us (6%)
  between operations  0.68 us (4%)
    pallas_call x1, Pallas kernels, local_part(): pl.pallas_call(functools.partial(local_kernel, zeros, cols, width, chunk)...  7.83 us
    pallas_call x1, Pallas kernels, per_device(): pl.pallas_call(functools.partial(most_kernel, zeros, cols, chunk), out_sh...  5.01 us
    pallas_call x2, Pallas kernels, per_device(): pl.pallas_call(functools.partial(last_kernel, zeros, chunk // 2, rows, fi...  3.18 us
    ppermute x3, starting transfers between devices, moved(): lax.ppermute(array, 'zero', [(i, zeros - 1 - i) for i in range(zeros)])  1.13 us
  transfers between devices with their start and end apart: 3, of which 0 were waited for; matrix products, arithmetic and copies ran while one was open for 0% of the time, Pallas kernels for 82%

profile of v3, /device:TPU:0, one launch (start us, length us, event | category | flops | bytes accessed | tf_op | source)
XLA Modules:
  0.0 17.9 jit_solution(4465509393163348043)
XLA Ops:
  0.6 0.6 %collective-permute-start = (bf16[1024,2048]{1,0:T(8,128)(2,1)}, bf16[1024,2048]{1,0:T(8,128)(2,1)S(1)}, u32[]{:S(2)}, u32[]{:S(2)}) collective-permute-start(bf16[1024,2048]{1,0:T(8,128)(2,1)} %gate_ref.1), channel_id=1, source_target_pairs={{0,4},{4,0},{1,5},{5,1},{2,6},{6,2},{3,7},{7,3},{8,12},{12,8},{9,1... | collective-permute-start | bytes 12582920 | tf_op jit(solution)/shard_map/ppermute | solution.py:371
  1.2 0.0 copy-start.1
  1.2 7.8 %shard_map.119 = (f32[1024,2048]{1,0:T(8,128)S(1)}, f32[1024,2048]{1,0:T(8,128)S(1)}, bf16[640,2048]{1,0:T(8,128)(2,1)S(1)}, bf16[384,2048]{1,0:T(8,128)(2,1)S(1...) custom-call(bf16[1024,2048]{1,0:T(8,128)(2,1)} %gate_ref.1, ...), custom_call_target="tpu_custom_call" | custom-call | flops 4294967296 | bytes 8388608 | tf_op jit(solution)/shard_map/pallas_call | solution.py:289
  9.0 0.3 %collective-permute-start.2 = (bf16[640,2048]{1,0:T(8,128)(2,1)S(1)}, bf16[640,2048]{1,0:T(8,128)(2,1)S(1)}, u32[]{:S(2)}, u32[]{:S(2)}) collective-permute-start(bf16[640,2048]{1,0:T(8,128)(2,1)S(1)} %get-tuple-element.30), channel_id=1, source_target_pairs={{0,4},{4,0},{1,5},{5,1},{2,6},{6,2},{3,7},{7,3},{8,12},{12,8},{9,1... | collective-permute-start | bytes 7864328 | tf_op jit(solution)/shard_map/ppermute | solution.py:371
  9.3 0.3 %collective-permute-start.1 = (bf16[384,2048]{1,0:T(8,128)(2,1)S(1)}, bf16[384,2048]{1,0:T(8,128)(2,1)S(1)}, u32[]{:S(2)}, u32[]{:S(2)}) collective-permute-start(bf16[384,2048]{1,0:T(8,128)(2,1)S(1)} %get-tuple-element.27), channel_id=1, source_target_pairs={{0,4},{4,0},{1,5},{5,1},{2,6},{6,2},{3,7},{7,3},{8,12},{12,8},{9,1... | collective-permute-start | bytes 4718600 | tf_op jit(solution)/shard_map/ppermute | solution.py:371
  9.6 0.0 collective-permute-done.moved
  9.6 0.0 copy-done.1
  9.6 0.0 copy-start
  9.6 5.0 %shard_map.120 = (bf16[2048,2048]{1,0:T(8,128)(2,1)}, bf16[2048,2048]{1,0:T(8,128)(2,1)}, f32[1,2048]{1,0:T(1,128)}, f32[1,2048]{1,0:T(1,128)}, bf16[16,128]{1,0...) custom-call(f32[1024,2048]{1,0:T(8,128)S(1)} %get-tuple-element.20.whole_gate, ...), custom_call_target="tpu_custom_call" | custom-call | flops 4294967296 | bytes 12582912 | tf_op jit(solution)/shard_map/pallas_call | solution.py:381
  14.6 0.0 collective-permute-done.2.moved
  14.6 0.0 copy-done
  14.7 1.8 %shard_map.121.up_in = bf16[2048,2048]{1,0:T(8,128)(2,1)} custom-call(bf16[640,2048]{1,0:T(8,128)(2,1)S(1)} %collective-permute-done.2.moved, bf16[1024,32]{1,0:T(8,128)(2,1)S(1)} %get-tuple-element.28.low_ref, bf16[32,2048]{1,0:T(8,128)(2,1)S(1)} %copy-done, f32[1,2048]{1,0:T(1,128)S(1)} %get-tuple-element.29.column_ref, ...), custom_call_target="tpu_custom_call", output_to_operand_aliasing={{}: (4, {})} | custom-call | flops 1073741824 | bytes 4194304 | tf_op jit(solution)/shard_map/pallas_call | solution.py:394
  16.4 0.0 collective-permute-done.1.moved
  16.5 1.4 %shard_map.122 = bf16[2048,2048]{1,0:T(8,128)(2,1)} custom-call(bf16[384,2048]{1,0:T(8,128)(2,1)S(1)} %collective-permute-done.1.moved, bf16[1024,32]{1,0:T(8,128)(2,1)S(1)} %get-tuple-element.28.low_ref, bf16[32,2048]{1,0:T(8,128)(2,1)S(1)} %copy-done, f32[1,2048]{1,0:T(1,128)S(1)} %get-tuple-element.29.column_ref, ...), custom_call_target="tpu_custom_call", output_to_operand_aliasing={{}: (4, {})} | custom-call | flops 1073741824 | bytes 4194304 | tf_op jit(solution)/shard_map/pallas_call | solution.py:394
Async XLA Ops:
  0.6 9.0 %collective-permute-start = (bf16[1024,2048]{1,0:T(8,128)(2,1)}, bf16[1024,2048]{1,0:T(8,128)(2,1)S(1)}, u32[]{:S(2)}, u32[]{:S(2)}) collective-permute-start(bf16[1024,2048]{1,0:T(8,128)(2,1)} %gate_ref.1), channel_id=1, source_target_pairs={{0,4},{4,0},{1,5},{5,1},{2,6},{6,2},{3,7},{7,3},{8,12},{12,8},{9,1... | collective-permute-start | bytes 12582920 | tf_op jit(solution)/shard_map/ppermute | solution.py:371
  1.2 8.4 %copy-start.1 = (bf16[32,2048]{1,0:T(8,128)(2,1)S(1)}, bf16[32,2048]{1,0:T(8,128)(2,1)}, u32[]{:S(2)}) copy-start(bf16[32,2048]{1,0:T(8,128)(2,1)} %high_ref.3) | copy-start | bytes 393220
  9.0 5.6 %collective-permute-start.2 = (bf16[640,2048]{1,0:T(8,128)(2,1)S(1)}, bf16[640,2048]{1,0:T(8,128)(2,1)S(1)}, u32[]{:S(2)}, u32[]{:S(2)}) collective-permute-start(bf16[640,2048]{1,0:T(8,128)(2,1)S(1)} %get-tuple-element.30), channel_id=1, source_target_pairs={{0,4},{4,0},{1,5},{5,1},{2,6},{6,2},{3,7},{7,3},{8,12},{12,8},{9,1... | collective-permute-start | bytes 7864328 | tf_op jit(solution)/shard_map/ppermute | solution.py:371
  9.3 7.1 %collective-permute-start.1 = (bf16[384,2048]{1,0:T(8,128)(2,1)S(1)}, bf16[384,2048]{1,0:T(8,128)(2,1)S(1)}, u32[]{:S(2)}, u32[]{:S(2)}) collective-permute-start(bf16[384,2048]{1,0:T(8,128)(2,1)S(1)} %get-tuple-element.27), channel_id=1, source_target_pairs={{0,4},{4,0},{1,5},{5,1},{2,6},{6,2},{3,7},{7,3},{8,12},{12,8},{9,1... | collective-permute-start | bytes 4718600 | tf_op jit(solution)/shard_map/ppermute | solution.py:371
  9.6 5.0 %copy-start = (bf16[32,2048]{1,0:T(8,128)(2,1)S(1)}, bf16[32,2048]{1,0:T(8,128)(2,1)}, u32[]{:S(2)}) copy-start(bf16[32,2048]{1,0:T(8,128)(2,1)} %high_ref.5) | copy-start | bytes 393220

commit v4 on v3

--- a/solution.py
+++ b/solution.py
@@ -327,8 +327,8 @@
 
 
 def most_kernel(zeros, cols, chunk, whole_gate, whole_up, moved, far_lows, high_ref, most, far_most, norm_in,
-                gate_out, up_out, column_gate_out, column_up_out, norm_out, low_up, column_up,
-                stage, low_gate, column_gate, norm, sems, line_sems):
+                gate_out, up_out, column_gate_out, column_up_out, norm_out, low_up, scale_up,
+                stage, low_gate, column_gate, column_up, norm, sems, line_sems):
     zero = lax.axis_index("zero")
     rows, columns = moved.shape
     near, far = zero * rows, (zeros - 1 - zero) * rows
@@ -336,6 +336,7 @@
         at = pl.ds(k * columns, columns)
         column[...] = jnp.maximum(most[:, at], far_most[:, at])
     scale = 1.0 / column_up[...]
+    scale_up[...] = scale
     copies = write_rows(lambda here: whole_up[here, :] * scale, chunk, stage.at[0], up_out, near, sems.at[0])
     gate_scale = 1.0 / column_gate[...]
     copies += write_rows(lambda here: whole_gate[here, :] * gate_scale, chunk, stage.at[1], gate_out, near, sems.at[1])
@@ -353,7 +354,7 @@
 
 def last_kernel(zeros, chunk, rows, first, moved, low_ref, high_ref, column_ref, up_in, up_out, stage, sems):
     zero = lax.axis_index("zero")
-    high, scale = high_ref[...] * jnp.bfloat16(mix_rate), 1.0 / column_ref[...]
+    high, scale = high_ref[...] * jnp.bfloat16(mix_rate), column_ref[...]
     for copy in write_rows(far_value(moved, low_ref, first, high, scale), chunk, stage, up_out,
                            (zeros - 1 - zero) * rows + first, sems):
         copy.wait()
@@ -385,7 +386,8 @@
         in_specs=[vmem] * 8,
         out_specs=[hbm] * 5 + [vmem] * 2,
         scratch_shapes=[pltpu.VMEM((3, rows, columns), jnp.bfloat16), pltpu.VMEM((rows, rank), low_gate.dtype),
-                        pltpu.VMEM((1, columns), jnp.float32), pltpu.VMEM((group * tall, lanes), jnp.bfloat16),
+                        pltpu.VMEM((1, columns), jnp.float32), pltpu.VMEM((1, columns), jnp.float32),
+                        pltpu.VMEM((group * tall, lanes), jnp.bfloat16),
                         pltpu.SemaphoreType.DMA((3, rows // chunk)), pltpu.SemaphoreType.DMA((3,))],
         cost_estimate=pl.CostEstimate(flops=2 ** 32, bytes_accessed=3 * 2 ** 22, transcendentals=0),
         compiler_params=pltpu.CompilerParams(vmem_limit_bytes=16 * 2 ** 20),

time: 18 us -> 18 us (level)
  no operation moved by 1% of the time
where the time goes in v4:
time: 18 us; the launch traced here: 17.9 us
  Pallas kernels  16 us (89%)
  starting transfers between devices  1.13 us (6%)
  between operations  0.68 us (4%)
    pallas_call x1, Pallas kernels, local_part(): pl.pallas_call(functools.partial(local_kernel, zeros, cols, width, chunk)...  7.83 us
    pallas_call x1, Pallas kernels, per_device(): pl.pallas_call(functools.partial(most_kernel, zeros, cols, chunk), out_sh...  5.02 us
    pallas_call x2, Pallas kernels, per_device(): pl.pallas_call(functools.partial(last_kernel, zeros, chunk // 2, rows, fi...  3.17 us
    ppermute x3, starting transfers between devices, moved(): lax.ppermute(array, 'zero', [(i, zeros - 1 - i) for i in range(zeros)])  1.13 us
  transfers between devices with their start and end apart: 3, of which 0 were waited for; matrix products, arithmetic and copies ran while one was open for 0% of the time, Pallas kernels for 82%

profile of v4, /device:TPU:0, one launch (start us, length us, event | category | flops | bytes accessed | tf_op | source)
XLA Modules:
  0.0 17.9 jit_solution(14958764020340357962)
XLA Ops:
  0.6 0.6 %collective-permute-start = (bf16[1024,2048]{1,0:T(8,128)(2,1)}, bf16[1024,2048]{1,0:T(8,128)(2,1)S(1)}, u32[]{:S(2)}, u32[]{:S(2)}) collective-permute-start(bf16[1024,2048]{1,0:T(8,128)(2,1)} %gate_ref.1), channel_id=1, source_target_pairs={{0,4},{4,0},{1,5},{5,1},{2,6},{6,2},{3,7},{7,3},{8,12},{12,8},{9,1... | collective-permute-start | bytes 12582920 | tf_op jit(solution)/shard_map/ppermute | solution.py:372
  1.2 0.0 copy-start.1
  1.2 7.8 %shard_map.119 = (f32[1024,2048]{1,0:T(8,128)S(1)}, f32[1024,2048]{1,0:T(8,128)S(1)}, bf16[640,2048]{1,0:T(8,128)(2,1)S(1)}, bf16[384,2048]{1,0:T(8,128)(2,1)S(1...) custom-call(bf16[1024,2048]{1,0:T(8,128)(2,1)} %gate_ref.1, ...), custom_call_target="tpu_custom_call" | custom-call | flops 4294967296 | bytes 8388608 | tf_op jit(solution)/shard_map/pallas_call | solution.py:289
  9.0 0.3 %collective-permute-start.2 = (bf16[640,2048]{1,0:T(8,128)(2,1)S(1)}, bf16[640,2048]{1,0:T(8,128)(2,1)S(1)}, u32[]{:S(2)}, u32[]{:S(2)}) collective-permute-start(bf16[640,2048]{1,0:T(8,128)(2,1)S(1)} %get-tuple-element.30), channel_id=1, source_target_pairs={{0,4},{4,0},{1,5},{5,1},{2,6},{6,2},{3,7},{7,3},{8,12},{12,8},{9,1... | collective-permute-start | bytes 7864328 | tf_op jit(solution)/shard_map/ppermute | solution.py:372
  9.3 0.3 %collective-permute-start.1 = (bf16[384,2048]{1,0:T(8,128)(2,1)S(1)}, bf16[384,2048]{1,0:T(8,128)(2,1)S(1)}, u32[]{:S(2)}, u32[]{:S(2)}) collective-permute-start(bf16[384,2048]{1,0:T(8,128)(2,1)S(1)} %get-tuple-element.27), channel_id=1, source_target_pairs={{0,4},{4,0},{1,5},{5,1},{2,6},{6,2},{3,7},{7,3},{8,12},{12,8},{9,1... | collective-permute-start | bytes 4718600 | tf_op jit(solution)/shard_map/ppermute | solution.py:372
  9.6 0.0 collective-permute-done.moved
  9.6 0.0 copy-done.1
  9.6 0.0 copy-start
  9.6 5.0 %shard_map.120 = (bf16[2048,2048]{1,0:T(8,128)(2,1)}, bf16[2048,2048]{1,0:T(8,128)(2,1)}, f32[1,2048]{1,0:T(1,128)}, f32[1,2048]{1,0:T(1,128)}, bf16[16,128]{1,0...) custom-call(f32[1024,2048]{1,0:T(8,128)S(1)} %get-tuple-element.20.whole_gate, ...), custom_call_target="tpu_custom_call" | custom-call | flops 4294967296 | bytes 12582912 | tf_op jit(solution)/shard_map/pallas_call | solution.py:382
  14.6 0.0 collective-permute-done.2.moved
  14.7 0.0 copy-done
  14.7 1.8 %shard_map.121.up_in = bf16[2048,2048]{1,0:T(8,128)(2,1)} custom-call(bf16[640,2048]{1,0:T(8,128)(2,1)S(1)} %collective-permute-done.2.moved, bf16[1024,32]{1,0:T(8,128)(2,1)S(1)} %get-tuple-element.28.low_ref, bf16[32,2048]{1,0:T(8,128)(2,1)S(1)} %copy-done, f32[1,2048]{1,0:T(1,128)S(1)} %get-tuple-element.29.column_ref, ...), custom_call_target="tpu_custom_call", output_to_operand_aliasing={{}: (4, {})} | custom-call | flops 1073741824 | bytes 4194304 | tf_op jit(solution)/shard_map/pallas_call | solution.py:396
  16.4 0.0 collective-permute-done.1.moved
  16.5 1.4 %shard_map.122 = bf16[2048,2048]{1,0:T(8,128)(2,1)} custom-call(bf16[384,2048]{1,0:T(8,128)(2,1)S(1)} %collective-permute-done.1.moved, bf16[1024,32]{1,0:T(8,128)(2,1)S(1)} %get-tuple-element.28.low_ref, bf16[32,2048]{1,0:T(8,128)(2,1)S(1)} %copy-done, f32[1,2048]{1,0:T(1,128)S(1)} %get-tuple-element.29.column_ref, ...), custom_call_target="tpu_custom_call", output_to_operand_aliasing={{}: (4, {})} | custom-call | flops 1073741824 | bytes 4194304 | tf_op jit(solution)/shard_map/pallas_call | solution.py:396
Async XLA Ops:
  0.6 9.0 %collective-permute-start = (bf16[1024,2048]{1,0:T(8,128)(2,1)}, bf16[1024,2048]{1,0:T(8,128)(2,1)S(1)}, u32[]{:S(2)}, u32[]{:S(2)}) collective-permute-start(bf16[1024,2048]{1,0:T(8,128)(2,1)} %gate_ref.1), channel_id=1, source_target_pairs={{0,4},{4,0},{1,5},{5,1},{2,6},{6,2},{3,7},{7,3},{8,12},{12,8},{9,1... | collective-permute-start | bytes 12582920 | tf_op jit(solution)/shard_map/ppermute | solution.py:372
  1.2 8.4 %copy-start.1 = (bf16[32,2048]{1,0:T(8,128)(2,1)S(1)}, bf16[32,2048]{1,0:T(8,128)(2,1)}, u32[]{:S(2)}) copy-start(bf16[32,2048]{1,0:T(8,128)(2,1)} %high_ref.3) | copy-start | bytes 393220
  9.0 5.6 %collective-permute-start.2 = (bf16[640,2048]{1,0:T(8,128)(2,1)S(1)}, bf16[640,2048]{1,0:T(8,128)(2,1)S(1)}, u32[]{:S(2)}, u32[]{:S(2)}) collective-permute-start(bf16[640,2048]{1,0:T(8,128)(2,1)S(1)} %get-tuple-element.30), channel_id=1, source_target_pairs={{0,4},{4,0},{1,5},{5,1},{2,6},{6,2},{3,7},{7,3},{8,12},{12,8},{9,1... | collective-permute-start | bytes 7864328 | tf_op jit(solution)/shard_map/ppermute | solution.py:372
  9.3 7.1 %collective-permute-start.1 = (bf16[384,2048]{1,0:T(8,128)(2,1)S(1)}, bf16[384,2048]{1,0:T(8,128)(2,1)S(1)}, u32[]{:S(2)}, u32[]{:S(2)}) collective-permute-start(bf16[384,2048]{1,0:T(8,128)(2,1)S(1)} %get-tuple-element.27), channel_id=1, source_target_pairs={{0,4},{4,0},{1,5},{5,1},{2,6},{6,2},{3,7},{7,3},{8,12},{12,8},{9,1... | collective-permute-start | bytes 4718600 | tf_op jit(solution)/shard_map/ppermute | solution.py:372
  9.6 5.0 %copy-start = (bf16[32,2048]{1,0:T(8,128)(2,1)S(1)}, bf16[32,2048]{1,0:T(8,128)(2,1)}, u32[]{:S(2)}) copy-start(bf16[32,2048]{1,0:T(8,128)(2,1)} %high_ref.5) | copy-start | bytes 393220
